TPU v7x, 32 devices: a whole 2x2x4 slice. The times are simulated.
32 devices in a mesh: shard: 8 (over z, y), model: 4 (over x, core).
Axes of the slice: x: 2, y: 2, z: 4, core: 2. Of those that a mesh axis runs over, the one named last changes fastest.
Arguments:
- gradients: float32 [32, 128, 4096], P(None, 'shard', 'model'), may hold values from -6 to 6
- momentum: float32 [32, 128, 4096], P(None, 'shard', 'model'), may hold values from -6 to 6
- weights: float32 [32, 128, 4096], P(None, 'shard', 'model'), may hold values from -0.1875 to 0.1875
Outputs:
- new_weights: float32 [32, 128, 4096], P(None, 'shard', 'model')
- new_momentum: float32 [32, 128, 4096], P(None, 'shard', 'model')
All inputs are finite; a program needn't handle non-finite values.
Results may differ from a plain program's by a relative error of at most 0.00015.
Values sent between devices are 32-bit elements; how exact they have to be, the bound alone decides.
No kernel may reach another device: no remote copies, remote signals or barrier semaphores. Data moves between devices by JAX's collectives and lax.ppermute only.
A program may use at most 128 MiB of HBM per device.

v0:
```python
import jax
import jax.numpy as jnp
from jax import lax
from jax.sharding import PartitionSpec as P

ITERS = 4
hold_rate = 0.8
learn_rate = 1.0
HIGH = lax.Precision.HIGHEST


def mul(a, b):
    return jnp.einsum("mij,mjk->mik", a, b, precision=HIGH)


def direction(gram):
    eye = jnp.eye(gram.shape[-1], dtype=gram.dtype)
    squares = jnp.sum(gram * eye, axis=(1, 2), keepdims=True)
    scale = lax.rsqrt(squares + 1e-06)
    a = gram * scale * scale
    total = None
    for step in range(ITERS):
        q = 3.4445 * eye - 4.775 * a + 2.0315 * mul(a, a)
        total = q if total is None else mul(q, total)
        if step < ITERS - 1:
            a = mul(mul(q, a), q)
    return total * scale


def make(mesh):
    models = mesh.shape["model"]

    def on_device(gradients, momentum, weights):
        new_momentum = hold_rate * momentum + gradients
        whole = lax.all_to_all(new_momentum, "shard", split_axis=0, concat_axis=1, tiled=True)
        gram = jnp.einsum("mik,mjk->mij", whole, whole, precision=HIGH)
        mine = gram.shape[0] // models
        parts = lax.all_to_all(gram, "model", split_axis=0, concat_axis=0, tiled=True)
        gram = jnp.sum(parts.reshape(models, mine, *gram.shape[1:]), axis=0)
        turn = lax.all_gather(direction(gram), "model", axis=0, tiled=True)
        moved = mul(turn, whole)
        back = lax.all_to_all(moved, "shard", split_axis=1, concat_axis=0, tiled=True)
        new_weights = weights - learn_rate * back
        return (new_weights, new_momentum)

    return on_device


def solution(mesh):
    placed = P(None, "shard", "model")
    return jax.shard_map(
        make(mesh),
        mesh=mesh,
        in_specs=(placed, placed, placed),
        out_specs=(placed, placed),
        check_vma=False,
    )
```

profile of v0, /device:TPU:0, one launch (start us, length us, event | category | flops | bytes accessed | tf_op | source)
XLA Modules:
  0.0 138.1 jit_solution(6963360470699167812)
XLA Ops:
  0.6 2.7 %multiply_add_fusion = f32[32,16,1024]{2,1,0:T(8,128)S(1)} fusion(f32[32,16,1024]{2,1,0:T(8,128)} %param.3, f32[32,16,1024]{2,1,0:T(8,128)} %param.4), kind=kLoop, calls=%fused_computation.1 | loop fusion | flops 1048576 | bytes 6291456 | tf_op jit(solution)/shard_map/add | solution.py:34
  3.3 0.0 copy-start
  3.3 55.3 %all_to_all.41 = f32[32,16,1024]{2,1,0:T(8,128)S(1)} all-to-all(f32[32,16,1024]{2,1,0:T(8,128)S(1)} %multiply_add_fusion), channel_id=1, replica_groups=mesh['shard'=8,'model'=4] {'shard'}, dimensions={0} | all-to-all | bytes 4194304 | tf_op jit(solution)/shard_map/all_to_all | solution.py:35
  58.6 0.0 copy-done
  58.6 0.2 copy.7
  58.9 2.1 %fusion.7 = f32[4,128,128]{2,1,0:T(8,128)S(1)} fusion(f32[4,128,1024]{2,1,0:T(8,128)S(1)} %bitcast.37), kind=kOutput, calls=%fused_computation.21 | convolution fusion | flops 805306368 | bytes 2359296 | tf_op jit(solution)/shard_map/mik,mjk->mij/dot_general | solution.py:36
  60.9 8.6 %all_to_all.42 = f32[4,128,128]{2,1,0:T(8,128)S(1)} all-to-all(f32[4,128,128]{2,1,0:T(8,128)S(1)} %fusion.7), channel_id=1, replica_groups=mesh['shard'=8,'model'=4] {'model'}, dimensions={0} | all-to-all | bytes 524288 | tf_op jit(solution)/shard_map/all_to_all | solution.py:38
  69.5 0.6 select_reduce_fusion
  70.8 0.2 fusion.3
  71.1 0.2 fusion.4
  71.3 0.2 fusion.8
  71.5 0.2 fusion.2
  71.7 0.2 fusion.13
  71.9 0.2 fusion.9
  72.1 0.2 fusion.10
  72.3 0.2 fusion.1
  72.5 0.2 fusion.11
  72.8 0.2 fusion.14
  73.0 0.2 fusion.12
  73.2 0.2 fusion
  73.4 0.2 convolution_multiply_fusion
  73.6 5.8 %all-gather = f32[512,128]{1,0:T(8,128)S(1)} all-gather(f32[128,128]{1,0:T(8,128)S(1)} %convolution_multiply_fusion), channel_id=2, replica_groups=mesh['shard'=8,'model'=4] {'model'}, dimensions={0}, use_global_device_ids=true | all-gather | bytes 327680 | tf_op jit(solution)/shard_map/all_gather | solution.py:40
  79.4 1.9 %fusion.15 = f32[4,128,1024]{2,1,0:T(8,128)S(1)} fusion(f32[4,128,128]{2,1,0:T(8,128)S(1)} %bitcast.41, f32[4,128,1024]{2,1,0:T(8,128)S(1)} %bitcast.38), kind=kOutput, calls=%fused_computation.29 | convolution fusion | flops 805306368 | bytes 4456448 | tf_op jit(solution)/shard_map/mij,mjk->mik/dot_general | solution.py:13
  81.3 1.4 copy.8
  82.7 52.1 %all_to_all.43 = f32[4,128,1024]{2,0,1:T(4,128)S(1)} all-to-all(f32[4,128,1024]{2,0,1:T(4,128)S(1)} %copy.8), channel_id=1, replica_groups=mesh['shard'=8,'model'=4] {'shard'}, dimensions={1} | all-to-all | bytes 4194304 | tf_op jit(solution)/shard_map/all_to_all | solution.py:42
  134.8 0.0 copy-start.1
  134.8 1.2 copy.9
  136.0 0.4 copy-done.1
  136.3 1.7 %bitcast_subtract_fusion = f32[32,16,1024]{2,1,0:T(8,128)} fusion(f32[32,16,1024]{2,1,0:T(8,128)S(1)} %copy-done.1, f32[8,4,16,1024]{3,2,1,0:T(8,128)S(1)} %copy.9), kind=kLoop, calls=%fused_computation | loop fusion | flops 524288 | bytes 6291456 | tf_op jit(solution)/shard_map/sub | solution.py:43
  (1 shorter events, 0.0 us)
Async XLA Ops:
  3.3 55.4 %copy-start = (f32[32,16,1024]{2,1,0:T(8,128)}, f32[32,16,1024]{2,1,0:T(8,128)S(1)}, u32[]{:S(2)}) copy-start(f32[32,16,1024]{2,1,0:T(8,128)S(1)} %multiply_add_fusion) | copy-start | bytes 6291460
  134.8 1.6 %copy-start.1 = (f32[32,16,1024]{2,1,0:T(8,128)S(1)}, f32[32,16,1024]{2,1,0:T(8,128)}, u32[]{:S(2)}) copy-start(f32[32,16,1024]{2,1,0:T(8,128)} %param.5) | copy-start | bytes 6291460
where the time goes:
time: 138 us
  blocking collectives  122 us (88%)
  matrix products  6.62 us (5%)
  other arithmetic  5.03 us (4%)
  local copies, waits for them, and re-layouts  3.18 us (2%)
  between operations  1.48 us (1%)
    all_to_all x1, blocking collectives, on_device(): lax.all_to_all(new_momentum, 'shard', split_axis=0, concat_axis=1, tiled=...  55.3 us
    all_to_all x1, blocking collectives, on_device(): lax.all_to_all(moved, 'shard', split_axis=1, concat_axis=0, tiled=True)  52.1 us
    all_to_all x1, blocking collectives, on_device(): lax.all_to_all(gram, 'model', split_axis=0, concat_axis=0, tiled=True)  8.57 us
    all_gather x1, blocking collectives, on_device(): turn = lax.all_gather(direction(gram), 'model', axis=0, tiled=True)  5.78 us
    dot_general x14, matrix products, mul(): return jnp.einsum('mij,mjk->mik', a, b, precision=HIGH)  4.57 us

commit v1 on v0

--- a/solution.py
+++ b/solution.py
@@ -39,7 +39,12 @@
         gram = jnp.sum(parts.reshape(models, mine, *gram.shape[1:]), axis=0)
         turn = lax.all_gather(direction(gram), "model", axis=0, tiled=True)
         moved = mul(turn, whole)
-        back = lax.all_to_all(moved, "shard", split_axis=1, concat_axis=0, tiled=True)
+        back = jnp.concatenate(
+            lax.all_to_all(
+                jnp.stack(jnp.split(moved, lax.axis_size("shard"), axis=1)), "shard", 0, 0
+            ),
+            axis=0,
+        )
         new_weights = weights - learn_rate * back
         return (new_weights, new_momentum)
 

time: 138 us -> 136 us (0.986)
  local copies, waits for them, and re-layouts: 3.18 us -> 0.41 us
where the time goes in v1:
time: 136 us
  blocking collectives  122 us (90%)
  matrix products  6.62 us (5%)
  other arithmetic  5.03 us (4%)
  between operations  1.54 us (1%)
    all_to_all x1, blocking collectives, on_device(): lax.all_to_all(new_momentum, 'shard', split_axis=0, concat_axis=1, tiled=...  55.3 us
    all_to_all x1, blocking collectives, on_device(): lax.all_to_all(jnp.stack(jnp.split(moved, lax.axis_size('shard'), axis=1)...  52.2 us
    all_to_all x1, blocking collectives, on_device(): lax.all_to_all(gram, 'model', split_axis=0, concat_axis=0, tiled=True)  8.57 us
    all_gather x1, blocking collectives, on_device(): turn = lax.all_gather(direction(gram), 'model', axis=0, tiled=True)  5.78 us
    dot_general x14, matrix products, mul(): return jnp.einsum('mij,mjk->mik', a, b, precision=HIGH)  4.57 us

profile of v1, /device:TPU:0, one launch (start us, length us, event | category | flops | bytes accessed | tf_op | source)
XLA Modules:
  0.0 135.5 jit_solution(16316558857402077298)
XLA Ops:
  0.6 2.7 %multiply_add_fusion = f32[32,16,1024]{2,1,0:T(8,128)S(1)} fusion(f32[32,16,1024]{2,1,0:T(8,128)} %param.3, f32[32,16,1024]{2,1,0:T(8,128)} %param.4), kind=kLoop, calls=%fused_computation.1 | loop fusion | flops 1048576 | bytes 6291456 | tf_op jit(solution)/shard_map/add | solution.py:34
  3.3 0.0 copy-start
  3.3 55.3 %all_to_all.28 = f32[32,16,1024]{2,1,0:T(8,128)S(1)} all-to-all(f32[32,16,1024]{2,1,0:T(8,128)S(1)} %multiply_add_fusion), channel_id=1, replica_groups=mesh['shard'=8,'model'=4] {'shard'}, dimensions={0} | all-to-all | bytes 4194304 | tf_op jit(solution)/shard_map/all_to_all | solution.py:35
  58.6 0.0 copy-done
  58.6 0.2 copy.5
  58.9 2.1 %fusion.15 = f32[4,128,128]{2,1,0:T(8,128)S(1)} fusion(f32[4,128,1024]{2,1,0:T(8,128)S(1)} %bitcast.66), kind=kOutput, calls=%fused_computation.37 | convolution fusion | flops 805306368 | bytes 2359296 | tf_op jit(solution)/shard_map/mik,mjk->mij/dot_general | solution.py:36
  60.9 8.6 %all_to_all.29 = f32[4,128,128]{2,1,0:T(8,128)S(1)} all-to-all(f32[4,128,128]{2,1,0:T(8,128)S(1)} %fusion.15), channel_id=1, replica_groups=mesh['shard'=8,'model'=4] {'model'}, dimensions={0} | all-to-all | bytes 524288 | tf_op jit(solution)/shard_map/all_to_all | solution.py:38
  69.5 0.6 select_reduce_fusion
  70.8 0.2 fusion.3
  71.1 0.2 fusion.12
  71.3 0.2 fusion.16
  71.5 0.2 fusion.2
  71.7 0.2 fusion.21
  71.9 0.2 fusion.17
  72.1 0.2 fusion.18
  72.3 0.2 fusion.1
  72.5 0.2 fusion.19
  72.8 0.2 fusion.22
  73.0 0.2 fusion.20
  73.2 0.2 fusion
  73.4 0.2 convolution_multiply_fusion
  73.6 5.8 %all-gather = f32[512,128]{1,0:T(8,128)S(1)} all-gather(f32[128,128]{1,0:T(8,128)S(1)} %convolution_multiply_fusion), channel_id=2, replica_groups=mesh['shard'=8,'model'=4] {'model'}, dimensions={0}, use_global_device_ids=true | all-gather | bytes 327680 | tf_op jit(solution)/shard_map/all_gather | solution.py:40
  79.4 1.9 %fusion.23 = f32[4,128,1024]{2,1,0:T(8,128)S(1)} fusion(f32[4,128,128]{2,1,0:T(8,128)S(1)} %bitcast.69, f32[4,128,1024]{2,1,0:T(8,128)S(1)} %bitcast.67), kind=kOutput, calls=%fused_computation.45 | convolution fusion | flops 805306368 | bytes 4456448 | tf_op jit(solution)/shard_map/mij,mjk->mik/dot_general | solution.py:13
  81.5 0.0 copy-start.1
  81.5 52.2 %all_to_all.30 = f32[8,4,16,1024]{3,2,1,0:T(8,128)S(1)} all-to-all(f32[8,4,16,1024]{3,2,1,0:T(8,128)S(1)} %fusion.4), channel_id=1, replica_groups=mesh['shard'=8,'model'=4] {'shard'}, dimensions={0} | all-to-all | bytes 4194304 | tf_op jit(solution)/shard_map/all_to_all | solution.py:43
  133.8 0.0 copy-done.1
  133.8 1.7 %bitcast_subtract_fusion = f32[32,16,1024]{2,1,0:T(8,128)} fusion(f32[32,16,1024]{2,1,0:T(8,128)S(1)} %copy-done.1, f32[8,4,16,1024]{3,2,1,0:T(8,128)S(1)} %all_to_all.30), kind=kLoop, calls=%fused_computation | loop fusion | flops 524288 | bytes 6291456 | tf_op jit(solution)/shard_map/sub | solution.py:48
  (9 shorter events, 0.2 us)
Async XLA Ops:
  3.3 55.4 %copy-start = (f32[32,16,1024]{2,1,0:T(8,128)}, f32[32,16,1024]{2,1,0:T(8,128)S(1)}, u32[]{:S(2)}) copy-start(f32[32,16,1024]{2,1,0:T(8,128)S(1)} %multiply_add_fusion) | copy-start | bytes 6291460
  81.5 52.2 %copy-start.1 = (f32[32,16,1024]{2,1,0:T(8,128)S(1)}, f32[32,16,1024]{2,1,0:T(8,128)}, u32[]{:S(2)}) copy-start(f32[32,16,1024]{2,1,0:T(8,128)} %param.5) | copy-start | bytes 6291460
